TPU v7x, 32 devices: a whole 2x2x4 slice. The times are simulated.
32 devices in a mesh: cells: 32 (over z, y, x, core).
Axes of the slice: x: 2, y: 2, z: 4, core: 2. Of those that a mesh axis runs over, the one named last changes fastest.
Arguments:
- field: float32 [9, 55, 32768], P(None, None, 'cells'), may hold values from -6 to 6
- cell_area: float32 [32768], P('cells'), may hold values from 0.5 to 2
- dv_edge: float32 [103424], P('cells'), may hold values from 0.6 to 1.6
- dc_edge: float32 [103424], P('cells'), may hold values from 0.6 to 1.6
- cells_on_edge: int32 [2, 103424], P(None, 'cells'), may hold values from 0 to 1407, as said below
- edges_on_cell: int32 [6, 32768], P(None, 'cells'), may hold values from 0 to 3231, as said below
- send_cells: int32 [6, 2048], P(None, 'cells'), may hold values from 0 to 1023
- level_coef: float32 [55], replicated, may hold values from 0.005 to 0.02
Outputs:
- tendency: float32 [9, 55, 32768], P(None, None, 'cells')
Inputs may be any that keep to these rules, and one draw needn't show every extreme that they name: `cells_on_edge`: the blocks tile one periodic hexagonal mesh, each a parallelogram of 64 by 16 cells; block b borders b + 1 and b - 1 along the first direction, b + 16 and b - 16 along the second, and b + 15 and b - 15 at one cell each, all modulo 32. Every edge with a cell in a block is listed once in that block, with the same dv_edge and dc_edge wherever it is listed, plus one extra entry that no cell names. Cells and edges are numbered in random order in each block. `edges_on_cell`: each cell names six distinct edges of its block.
All inputs are finite; a program needn't handle non-finite values.
Results may differ from a plain program's by a relative error of at most 0.00005.
Values sent between devices are 32-bit elements; how exact they have to be, the bound alone decides.
A program may use at most 128 MiB of HBM per device.

v0:
```python
import jax
import jax.numpy as jnp
from jax import lax
from jax.sharding import PartitionSpec as P

CELLS_Y = 16
BLOCK_ROW = 16


def from_behind(x, axis, by):
    devices = lax.axis_size(axis)
    return lax.ppermute(x, axis, [(i, (i + by) % devices) for i in range(devices)])


def widen(piece, length):
    return jnp.pad(piece, ((0, 0), (0, length - piece.shape[1])))


def shards(
    field, cell_area, dv_edge, dc_edge, cells_on_edge, edges_on_cell, send_cells, level_coef
):
    length = send_cells.shape[1]
    side = CELLS_Y
    fields_n = field.shape[0]
    levels_n = field.shape[1]
    cell_count = field.shape[2]
    edge_count = dv_edge.shape[0]
    ext_count = cell_count + 6 * length
    rows_n = fields_n * levels_n
    highest = lax.Precision.HIGHEST
    weight = dv_edge / dc_edge
    first_end = jnp.take(cells_on_edge[0], edges_on_cell)
    own_index = lax.broadcasted_iota(jnp.int32, edges_on_cell.shape, 1)
    orient = jnp.where(first_end == own_index, 1.0, -1.0).astype(jnp.float32)
    cell_ids = lax.broadcasted_iota(jnp.int32, (cell_count, 6 * length), 0)
    selector = (cell_ids == send_cells.reshape(1, 6 * length)).astype(jnp.float32)
    ext_ids = lax.broadcasted_iota(jnp.int32, (ext_count, edge_count), 0)
    differ = (
        (ext_ids == cells_on_edge[1][None, :]).astype(jnp.float32)
        - (ext_ids == cells_on_edge[0][None, :]).astype(jnp.float32)
    ) * weight[None, :]
    edge_ids = lax.broadcasted_iota(jnp.int32, (edge_count, cell_count), 0)
    collect = jnp.zeros((edge_count, cell_count), jnp.float32)
    for slot_j in range(6):
        collect = collect + jnp.where(
            edge_ids == edges_on_cell[slot_j][None, :], orient[slot_j][None, :], 0.0
        )
    collect = collect / cell_area[None, :]
    operator = jnp.dot(differ, collect, precision=highest, preferred_element_type=jnp.float32)

    def extend(values):
        picked = jnp.dot(
            values, selector, precision=highest, preferred_element_type=jnp.float32
        ).reshape(rows_n, 6, length)
        toward_right = picked[:, 0, :side]
        toward_left = picked[:, 1, :side]
        toward_upper = picked[:, 2, :]
        toward_lower = picked[:, 3, :]
        corner_upper = picked[:, 4, :1]
        corner_lower = picked[:, 5, :1]
        carried_back = from_behind(
            jnp.concatenate([toward_left, corner_upper], axis=1), "cells", -1
        )
        carried_fore = from_behind(
            jnp.concatenate([toward_right, corner_lower], axis=1), "cells", 1
        )
        from_right = carried_back[:, :side]
        from_left = carried_fore[:, :side]
        carried_up = from_behind(
            jnp.concatenate([toward_upper, carried_back[:, side:]], axis=1), "cells", BLOCK_ROW
        )
        carried_down = from_behind(
            jnp.concatenate([toward_lower, carried_fore[:, side:]], axis=1), "cells", -BLOCK_ROW
        )
        from_below = carried_up[:, :length]
        corner_below = carried_up[:, length:]
        from_above = carried_down[:, :length]
        corner_above = carried_down[:, length:]
        return jnp.concatenate(
            [
                values,
                widen(from_left, length),
                widen(from_right, length),
                from_below,
                from_above,
                widen(corner_below, length),
                widen(corner_above, length),
            ],
            axis=1,
        )

    def laplacian(values):
        extended = extend(values)
        return jnp.dot(extended, operator, precision=highest, preferred_element_type=jnp.float32)

    flat = field.reshape(rows_n, cell_count)
    first_pass = laplacian(flat)
    second_pass = laplacian(first_pass).reshape(fields_n, levels_n, cell_count)
    return -level_coef[None, :, None] * second_pass


def solution(mesh):
    return jax.shard_map(
        shards,
        mesh=mesh,
        in_specs=(
            P(None, None, "cells"),
            P("cells"),
            P("cells"),
            P("cells"),
            P(None, "cells"),
            P(None, "cells"),
            P(None, "cells"),
            P(),
        ),
        out_specs=P(None, None, "cells"),
        check_vma=False,
    )
```

profile of v0, /device:TPU:0, one launch (start us, length us, event | category | flops | bytes accessed | tf_op | source)
XLA Modules:
  0.0 232.5 jit_solution(10507549430930275740)
XLA Ops:
  0.0 1.8 reshape.23
  2.6 1.8 fusion.36
  4.4 1.1 copy.37
  7.6 6.0 %collective-permute-start.1 = (f32[495,17]{0,1:T(8,128)S(1)}, f32[495,17]{0,1:T(8,128)S(1)}, u32[]{:S(2)}, u32[]{:S(2)}) collective-permute-start(f32[495,17]{0,1:T(8,128)S(1)} %pad_maximum_fusion.5), channel_id=1, source_target_pairs={{0,31},{1,0},{2,1},{3,2},{4,3},{5,4},{6,5},{7,6},{8,7},{9,8},{10,9... | collective-permute-start | bytes 100988 | tf_op jit(solution)/shard_map/ppermute | solution.py:12
  17.3 34.3 %gather_fusion = s32[6144]{0:T(1024)S(1)} fusion(s32[3232]{0:T(1024)S(1)} %get-tuple-element.6, s32[6144]{0:T(1024)S(1)} %broadcast_clamp_fusion), kind=kCustom, calls=%fused_computation | custom fusion | bytes 73728 | tf_op jit(solution)/shard_map/jit(_take)/gather | solution.py:32
  51.7 11.6 %fusion.58 = f32[1408,3232]{1,0:T(8,128)} fusion(f32[3232]{0:T(1024)S(1)} %div.11, s32[3232]{0:T(1024)S(1)} %get-tuple-element.6, s32[3232]{0:T(1024)S(1)} %get-tuple-element.5), kind=kLoop, calls=%fused_computation.2.clone.2 | loop fusion | flops 27303936 | bytes 18241408 | tf_op jit(solution)/shard_map/dot_general | solution.py:49
  63.4 1.2 collective-permute-start.3
  64.6 1.9 collective-permute-start.2
  66.5 93.5 %fusion = f32[1408,1024]{1,0:T(8,128)} fusion(f32[1024]{0:T(1024)S(1)} %copy-done.6, f32[1024]{0:T(1024)S(1)} %bitcast.68, s32[1024]{0:T(1024)S(1)} %bitcast.65, f32[1024]{0:T(1024)S(1)} %bitcast.69, s32[1024]{0:T(1024)S(1)} %bitcast.66, f32[1024]{0:T(1024)S(1)} %bitcast.70, s32[1024]{0:T(1024)S(1)} %bitcast.64, f32[1024]{0:T(1024)S(1)} %bitcast.71, ...), kind=kOutput, calls=%fused_computation.1 | convolution fusion | flops 55978033152 | bytes 24023040 | tf_op jit(solution)/shard_map/dot_general | solution.py:49
  161.6 1.6 slice.179
  164.2 3.1 %concatenate.34 = f32[495,1408]{1,0:T(8,128)} concatenate(f32[495,1024]{1,0:T(8,128)S(1)} %reshape.23, f32[495,64]{1,0:T(8,128)S(1)} %pad.26.clone, f32[495,64]{1,0:T(8,128)S(1)} %pad.27.clone, f32[495,64]{1,0:T(8,128)S(1)} %copy.40, f32[495,64]{1,0:T(8,128)S(1)} %copy.41, f32[495,64]{1,0:T(8,128)S(1)} %pad.28.clone, f32[495,64]{1,0:T(8,128)S(1)} %pad.29.clone), dimensions={1} | concatenate | bytes 5575680 | tf_op jit(solution)/shard_map/concatenate | solution.py:79
  167.2 13.0 %fusion.44 = f32[495,1024]{1,0:T(8,128)S(1)} fusion(f32[495,1408]{1,0:T(8,128)} %concatenate.34, f32[1408,1024]{1,0:T(8,128)} %fusion), kind=kOutput, calls=%fused_computation.78 | convolution fusion | flops 8564244480 | bytes 10582528 | tf_op jit(solution)/shard_map/dot_general | solution.py:94
  180.2 1.7 fusion.34
  183.2 5.3 %collective-permute-start.5 = (f32[495,17]{1,0:T(8,128)}, f32[495,17]{1,0:T(8,128)S(1)}, u32[]{:S(2)}, u32[]{:S(2)}) collective-permute-start(f32[495,17]{1,0:T(8,128)} %copy.46), channel_id=1, source_target_pairs={{0,31},{1,0},{2,1},{3,2},{4,3},{5,4},{6,5},{7,6},{8,7},{9,8},{10,9... | collective-permute-start | bytes 100988 | tf_op jit(solution)/shard_map/ppermute | solution.py:12
  188.6 2.9 %collective-permute-done.4 = f32[495,17]{1,0:T(8,128)S(1)} collective-permute-done((f32[495,17]{1,0:T(8,128)S(1)}, f32[495,17]{1,0:T(8,128)S(1)}, u32[]{:S(2)}, u32[]{:S(2)}) %collective-permute-start.4) | collective-permute-done | bytes 33692 | tf_op jit(solution)/shard_map/ppermute | solution.py:12
  191.8 1.2 collective-permute-done.5
  193.3 11.7 %collective-permute-start.6 = (f32[495,65]{1,0:T(8,128)S(1)}, f32[495,65]{1,0:T(8,128)S(1)}, u32[]{:S(2)}, u32[]{:S(2)}) collective-permute-start(f32[495,65]{1,0:T(8,128)S(1)} %pad_maximum_fusion), channel_id=1, source_target_pairs={{0,16},{1,17},{2,18},{3,19},{4,20},{5,21},{6,22},{7,23},{8,24},{9,... | collective-permute-start | bytes 386108 | tf_op jit(solution)/shard_map/ppermute | solution.py:12
  205.0 1.2 neg.4
  206.3 3.1 %collective-permute-done.7 = f32[495,65]{1,0:T(8,128)S(1)} collective-permute-done((f32[495,65]{1,0:T(8,128)S(1)}, f32[495,65]{1,0:T(8,128)S(1)}, u32[]{:S(2)}, u32[]{:S(2)}) %collective-permute-start.7) | collective-permute-done | bytes 128732 | tf_op jit(solution)/shard_map/ppermute | solution.py:12
  209.6 2.6 %collective-permute-done.6 = f32[495,65]{1,0:T(8,128)S(1)} collective-permute-done((f32[495,65]{1,0:T(8,128)S(1)}, f32[495,65]{1,0:T(8,128)S(1)}, u32[]{:S(2)}, u32[]{:S(2)}) %collective-permute-start.6) | collective-permute-done | bytes 128732 | tf_op jit(solution)/shard_map/ppermute | solution.py:12
  212.3 3.3 %concatenate.39 = f32[495,1408]{1,0:T(8,128)} concatenate(f32[495,1024]{1,0:T(8,128)S(1)} %fusion.44, f32[495,64]{1,0:T(8,128)S(1)} %pad.30, f32[495,64]{1,0:T(8,128)S(1)} %pad.31, f32[495,64]{1,0:T(8,128)S(1)} %bitcast.60, f32[495,64]{1,0:T(8,128)S(1)} %bitcast.58, f32[495,64]{1,0:T(8,128)S(1)} %pad.32, f32[495,64]{1,0:T(8,128)S(1)} %pad.33), dimensions={1} | concatenate | bytes 5575680 | tf_op jit(solution)/shard_map/concatenate | solution.py:79
  215.6 13.6 %fusion.45 = f32[495,1024]{1,0:T(8,128)} fusion(f32[495,1408]{1,0:T(8,128)} %concatenate.39, f32[1408,1024]{1,0:T(8,128)} %fusion), kind=kOutput, calls=%fused_computation.79 | convolution fusion | flops 8564244480 | bytes 10582528 | tf_op jit(solution)/shard_map/dot_general | solution.py:94
  229.2 1.8 reshape.26
  231.0 1.6 broadcast_multiply_fusion
  (74 shorter events, 11.4 us)
Async XLA Ops:
  2.6 49.1 %copy-start.1 = (s32[384]{0:T(512)}, s32[384]{0:T(512)S(1)}, u32[]{:S(2)}) copy-start(s32[384]{0:T(512)S(1)} %eq.93) | copy-start | bytes 4612
  7.1 56.3 %collective-permute-start = (f32[495,17]{0,1:T(8,128)S(1)}, f32[495,17]{0,1:T(8,128)S(1)}, u32[]{:S(2)}, u32[]{:S(2)}) collective-permute-start(f32[495,17]{0,1:T(8,128)S(1)} %pad_maximum_fusion.4), channel_id=1, source_target_pairs={{0,1},{1,2},{2,3},{3,4},{4,5},{5,6},{6,7},{7,8},{8,9},{9,10},{10,1... | collective-permute-start | bytes 100988 | tf_op jit(solution)/shard_map/ppermute | solution.py:12
  7.6 57.0 %collective-permute-start.1 = (f32[495,17]{0,1:T(8,128)S(1)}, f32[495,17]{0,1:T(8,128)S(1)}, u32[]{:S(2)}, u32[]{:S(2)}) collective-permute-start(f32[495,17]{0,1:T(8,128)S(1)} %pad_maximum_fusion.5), channel_id=1, source_target_pairs={{0,31},{1,0},{2,1},{3,2},{4,3},{5,4},{6,5},{7,6},{8,7},{9,8},{10,9... | collective-permute-start | bytes 100988 | tf_op jit(solution)/shard_map/ppermute | solution.py:12
  17.3 34.4 %copy-start = (s32[6,1024]{1,0:T(8,128)S(1)}, s32[6,1024]{1,0:T(8,128)}, u32[]{:S(2)}) copy-start(s32[6,1024]{1,0:T(8,128)} %param.13) | copy-start | bytes 73732
  17.3 34.4 %copy-start.3 = (f32[3232]{0:T(1024)S(1)}, f32[3232]{0:T(1024)}, u32[]{:S(2)}) copy-start(f32[3232]{0:T(1024)} %param.10) | copy-start | bytes 38788
  17.3 34.4 %copy-start.4 = (f32[3232]{0:T(1024)S(1)}, f32[3232]{0:T(1024)}, u32[]{:S(2)}) copy-start(f32[3232]{0:T(1024)} %param.11) | copy-start | bytes 38788
  51.6 14.9 %copy-start.6 = (f32[1024]{0:T(1024)S(1)}, f32[1024]{0:T(1024)}, u32[]{:S(2)}) copy-start(f32[1024]{0:T(1024)} %param.9) | copy-start | bytes 12292
  63.4 96.9 %collective-permute-start.3 = (f32[495,65]{0,1:T(8,128)S(1)}, f32[495,65]{0,1:T(8,128)S(1)}, u32[]{:S(2)}, u32[]{:S(2)}) collective-permute-start(f32[495,65]{0,1:T(8,128)S(1)} %pad_maximum_fusion.3), channel_id=1, source_target_pairs={{0,16},{1,17},{2,18},{3,19},{4,20},{5,21},{6,22},{7,23},{8,24},{9,... | collective-permute-start | bytes 386108 | tf_op jit(solution)/shard_map/ppermute | solution.py:12
  64.6 96.0 %collective-permute-start.2 = (f32[495,65]{0,1:T(8,128)S(1)}, f32[495,65]{0,1:T(8,128)}, u32[]{:S(2)}, u32[]{:S(2)}) collective-permute-start(f32[495,65]{0,1:T(8,128)S(1)} %pad_maximum_fusion.2), channel_id=1, source_target_pairs={{0,16},{1,17},{2,18},{3,19},{4,20},{5,21},{6,22},{7,23},{8,24},{9,... | collective-permute-start | bytes 386108 | tf_op jit(solution)/shard_map/ppermute | solution.py:12
  167.2 13.0 %copy-start.2 = (s32[384]{0:T(512)S(1)}, s32[384]{0:T(512)}, u32[]{:S(2)}) copy-start(s32[384]{0:T(512)} %copy-done.1) | copy-start | bytes 4612
  182.1 9.4 %collective-permute-start.4 = (f32[495,17]{1,0:T(8,128)S(1)}, f32[495,17]{1,0:T(8,128)S(1)}, u32[]{:S(2)}, u32[]{:S(2)}) collective-permute-start(f32[495,17]{1,0:T(8,128)S(1)} %copy.45), channel_id=1, source_target_pairs={{0,1},{1,2},{2,3},{3,4},{4,5},{5,6},{6,7},{7,8},{8,9},{9,10},{10,1... | collective-permute-start | bytes 100988 | tf_op jit(solution)/shard_map/ppermute | solution.py:12
  183.2 9.9 %collective-permute-start.5 = (f32[495,17]{1,0:T(8,128)}, f32[495,17]{1,0:T(8,128)S(1)}, u32[]{:S(2)}, u32[]{:S(2)}) collective-permute-start(f32[495,17]{1,0:T(8,128)} %copy.46), channel_id=1, source_target_pairs={{0,31},{1,0},{2,1},{3,2},{4,3},{5,4},{6,5},{7,6},{8,7},{9,8},{10,9... | collective-permute-start | bytes 100988 | tf_op jit(solution)/shard_map/ppermute | solution.py:12
  191.8 17.7 %collective-permute-start.7 = (f32[495,65]{1,0:T(8,128)S(1)}, f32[495,65]{1,0:T(8,128)S(1)}, u32[]{:S(2)}, u32[]{:S(2)}) collective-permute-start(f32[495,65]{1,0:T(8,128)S(1)} %pad_maximum_fusion.1), channel_id=1, source_target_pairs={{0,16},{1,17},{2,18},{3,19},{4,20},{5,21},{6,22},{7,23},{8,24},{9,... | collective-permute-start | bytes 386108 | tf_op jit(solution)/shard_map/ppermute | solution.py:12
  193.3 18.8 %collective-permute-start.6 = (f32[495,65]{1,0:T(8,128)S(1)}, f32[495,65]{1,0:T(8,128)S(1)}, u32[]{:S(2)}, u32[]{:S(2)}) collective-permute-start(f32[495,65]{1,0:T(8,128)S(1)} %pad_maximum_fusion), channel_id=1, source_target_pairs={{0,16},{1,17},{2,18},{3,19},{4,20},{5,21},{6,22},{7,23},{8,24},{9,... | collective-permute-start | bytes 386108 | tf_op jit(solution)/shard_map/ppermute | solution.py:12
  215.6 15.4 %copy-start.5 = (f32[55]{0:T(128)S(1)}, f32[55]{0:T(128)}, u32[]{:S(2)}) copy-start(f32[55]{0:T(128)} %neg.4) | copy-start | bytes 664
where the time goes:
time: 233 us
  matrix products  124 us (53%)
  local copies, waits for them, and re-layouts  56.5 us (24%)
  starting transfers between devices  26.7 us (11%)
  other arithmetic  15.6 us (7%)
  waiting for transfers between devices  9.76 us (4%)
    dot_general x1, matrix products, shards(): jnp.dot(differ, collect, precision=highest, preferred_element_type=jnp.fl...  93.5 us
    gather x2, local copies, waits for them, and re-layouts, shards(): first_end = jnp.take(cells_on_edge[0], edges_on_cell)  34.3 us
    ppermute x8, starting transfers between devices, from_behind(): lax.ppermute(x, axis, [(i, (i + by) % devices) for i in range(devices)])  26.7 us
    dot_general x2, matrix products, laplacian(): jnp.dot(extended, operator, precision=highest, preferred_element_type=jnp...  26.6 us
    dot_general x1, other arithmetic, shards(): jnp.dot(differ, collect, precision=highest, preferred_element_type=jnp.fl...  11.6 us
    ppermute x8, waiting for transfers between devices, from_behind(): lax.ppermute(x, axis, [(i, (i + by) % devices) for i in range(devices)])  9.76 us
    concatenate x2, local copies, waits for them, and re-layouts, extend(): jnp.concatenate([values, widen(from_left, length), widen(from_right, leng...  6.37 us
  transfers between devices with their start and end apart: 8, of which 4 were waited for; matrix products, arithmetic and copies ran while one was open for 63% of the time, Pallas kernels for 0%

commit v1 on v0

v1 whole, which is shorter than its diff:
```python
import functools

import jax
import jax.numpy as jnp
from jax import lax
from jax.experimental import pallas as pl
from jax.experimental.pallas import tpu as pltpu
from jax.sharding import PartitionSpec as P

CELLS_Y = 16
BLOCK_ROW = 16
OFFSETS = (1, -1, BLOCK_ROW, -BLOCK_ROW, BLOCK_ROW - 1, 1 - BLOCK_ROW)
LANES = 128
CHUNKS = 2


def up(value, step):
    return -(-value // step) * step


def slots(length):
    side = CELLS_Y
    counts = (side, side, length, length, 8, 8)
    order = (2, 3, 0, 1, 4, 5)
    base = [0] * 6
    at = 0
    for k in order:
        base[k] = at
        at += counts[k]
    return tuple(base), counts, at


def prepare_kernel(
    dv_ref, dc_ref, ends_ref, edges_ref, send_ref, area_ref, near_ref, coef_ref, cols_ref,
    weight, packed, index,
):
    edge_count = dv_ref.shape[1]
    cell_count = edges_ref.shape[1]
    length = send_ref.shape[1]
    base, counts, _ = slots(length)
    tables = weight.shape[1] // LANES
    weight[...] = jnp.zeros_like(weight)
    packed[...] = jnp.zeros_like(packed)
    index[...] = jnp.zeros_like(index)
    weight[:, :edge_count] = dv_ref[...] / dc_ref[...]
    packed[:, :edge_count] = ends_ref[0:1, :] + ends_ref[1:2, :] * 4096
    index[0:6, :] = edges_ref[...]
    row = lax.broadcasted_iota(jnp.int32, (8, LANES), 0)
    lane = lax.broadcasted_iota(jnp.int32, (8, LANES), 1)
    for tile in range(cell_count // LANES):
        here = slice(tile * LANES, (tile + 1) * LANES)
        wanted = index[:, here]
        high = wanted >> 7
        low = wanted & 127
        w = jnp.zeros((8, LANES), jnp.float32)
        p = jnp.zeros((8, LANES), jnp.int32)
        for k in range(tables):
            part = slice(k * LANES, (k + 1) * LANES)
            wk = jnp.broadcast_to(weight[0:1, part], (8, LANES))
            pk = jnp.broadcast_to(packed[0:1, part], (8, LANES))
            hit = high == k
            w = jnp.where(hit, jnp.take_along_axis(wk, low, axis=1), w)
            p = jnp.where(hit, jnp.take_along_axis(pk, low, axis=1), p)
        first = p & 4095
        second = p >> 12
        other = jnp.where(first == lane + tile * LANES, second, first)
        away = other - cell_count
        place = jnp.zeros((8, LANES), jnp.int32)
        for k in range(6):
            inside = (away >= k * length) & (away < (k + 1) * length)
            place = jnp.where(inside, away - k * length + base[k], place)
        near = jnp.where(away < 0, other, cell_count + place)
        share = w / area_ref[0:1, here]
        share = jnp.where(row < 6, share, 0.0)
        total = jnp.sum(share, axis=0, keepdims=True)
        near_ref[:, here] = jnp.where(row < 6, near, -1)
        coef_ref[:, here] = jnp.where(row == 6, total, share)
    for k in range(6):
        rows = lax.broadcasted_iota(jnp.int32, (counts[k], length), 0)
        columns = lax.broadcasted_iota(jnp.int32, (counts[k], length), 1)
        ids = send_ref[k : k + 1, :].astype(jnp.float32)
        column = jnp.sum(jnp.where(rows == columns, ids, 0.0), axis=1, keepdims=True)
        cols_ref[base[k] : base[k] + counts[k], :] = jnp.broadcast_to(
            column, (counts[k], LANES)
        ).astype(jnp.int32)


def split(values):
    high = values.astype(jnp.bfloat16)
    low = (values - high.astype(jnp.float32)).astype(jnp.bfloat16)
    return high, low


def main_kernel(
    devices, length, field_ref, near_ref, coef_ref, cols_ref, out_ref,
    landed, flat, first, matrix, rim, triple, selector, outgoing, incoming,
    load_sem, send_sem, recv_sem,
):
    fields_n, levels_n, cell_count = field_ref.shape
    stride = up(levels_n, 8)
    chunk = flat.shape[0] // CHUNKS
    halo = rim.shape[0] // 3
    base, counts, used = slots(length)
    me = lax.axis_index("cells")
    targets = [lax.rem(me + (o + devices), devices) for o in OFFSETS]

    loads = [
        pltpu.make_async_copy(field_ref.at[f], landed.at[f], load_sem.at[f])
        for f in range(fields_n)
    ]
    for load in loads:
        load.start()

    barrier = pltpu.get_barrier_semaphore()
    for target in targets:
        pl.semaphore_signal(
            barrier, inc=1, device_id=(target,), device_id_type=pl.DeviceIdType.MESH
        )

    lane = lax.broadcasted_iota(jnp.int32, (used, LANES), 1)
    for tile in range(cell_count // LANES):
        hit = cols_ref[...] == lane + tile * LANES
        ones = jnp.where(hit, 1.0, 0.0).astype(jnp.bfloat16)
        selector[:, tile * LANES : (tile + 1) * LANES] = ones
        at = cell_count + tile * LANES
        selector[:, at : at + LANES] = ones
    for lap in range(2):
        for c in range(CHUNKS):
            incoming[lap, c, used:, :] = jnp.zeros((halo - used, chunk), jnp.float32)
    rows = flat.shape[0]
    end = fields_n * stride
    if rows > end:
        flat[end:, :] = jnp.zeros((rows - end, cell_count), jnp.float32)
    if stride > levels_n:
        for f in range(fields_n):
            at = (f + 1) * stride - 8
            flat[at : at + 8, :] = jnp.zeros((8, cell_count), jnp.float32)

    def spread(values, c):
        high, low = split(values)
        triple[c, :, :cell_count] = high
        triple[c, :, cell_count : 2 * cell_count] = low
        triple[c, :, 2 * cell_count :] = high

    def copies(lap, c):
        return [
            pltpu.make_async_remote_copy(
                src_ref=outgoing.at[lap, c, pl.ds(base[k], counts[k])],
                dst_ref=incoming.at[lap, c, pl.ds(base[k], counts[k])],
                send_sem=send_sem.at[lap, c, k],
                recv_sem=recv_sem.at[lap, c, k],
                device_id=(targets[k],),
                device_id_type=pl.DeviceIdType.MESH,
            )
            for k in (2, 3, 4, 5, 0, 1)
        ]

    def send(lap, c):
        outgoing[lap, c] = lax.dot_general(
            selector[...],
            triple[c, :, : 2 * cell_count],
            (((1,), (1,)), ((), ())),
            preferred_element_type=jnp.float32,
        )
        for copy in copies(lap, c):
            copy.start()

    def own(c):
        return jnp.dot(triple[c], matrix[...], preferred_element_type=jnp.float32)

    def outside(lap, c):
        for copy in copies(lap, c):
            copy.wait_recv()
        high, low = split(incoming[lap, c].T)
        lhs = jnp.concatenate([high, low, high], axis=1)
        return jnp.dot(lhs, rim[...], preferred_element_type=jnp.float32)

    loaded = 0
    for c in range(CHUNKS):
        need = min(fields_n, -(-((c + 1) * chunk) // stride))
        for f in range(loaded, need):
            loads[f].wait()
            flat[f * stride : f * stride + levels_n, :] = landed[f]
        loaded = max(loaded, need)
        spread(flat[c * chunk : (c + 1) * chunk, :], c)
        if c == 0:
            pl.semaphore_wait(barrier, len(targets))
        send(0, c)

    ids = lax.broadcasted_iota(jnp.int32, (LANES, LANES), 0)

    def entries(start, tile):
        here = slice(tile * LANES, (tile + 1) * LANES)
        block = jnp.zeros((LANES, LANES), jnp.float32)
        for j in range(6):
            hit = ids == near_ref[j : j + 1, here] - start
            block = jnp.where(hit, coef_ref[j : j + 1, here], block)
        return split(block)

    def fill(r, carry):
        start = pl.multiple_of(r * LANES, LANES)
        for tile in range(cell_count // LANES):
            here = slice(tile * LANES, (tile + 1) * LANES)
            high, low = entries(start, tile)
            matrix[pl.ds(start, LANES), here] = high
            matrix[pl.ds(start + cell_count, LANES), here] = high
            matrix[pl.ds(start + 2 * cell_count, LANES), here] = low
        return carry

    lax.fori_loop(0, cell_count // LANES, fill, 0)
    for r in range(halo // LANES):
        for tile in range(cell_count // LANES):
            here = slice(tile * LANES, (tile + 1) * LANES)
            high, low = entries(cell_count + r * LANES, tile)
            rim[r * LANES : (r + 1) * LANES, here] = high
            rim[halo + r * LANES : halo + (r + 1) * LANES, here] = high
            rim[2 * halo + r * LANES : 2 * halo + (r + 1) * LANES, here] = low

    for c in range(CHUNKS):
        part = slice(c * chunk, (c + 1) * chunk)
        first[part, :] = own(c) - flat[part, :] * coef_ref[6:7, :]
        result = first[part, :] + outside(0, c)
        first[part, :] = result
        spread(result, c)
        send(1, c)
    for c in range(CHUNKS):
        part = slice(c * chunk, (c + 1) * chunk)
        out_ref[part, :] = own(c) - first[part, :] * coef_ref[6:7, :]
        out_ref[part, :] = out_ref[part, :] + outside(1, c)
    for lap in range(2):
        for c in range(CHUNKS):
            for copy in copies(lap, c):
                copy.wait_send()


def shards(
    devices, field, cell_area, dv_edge, dc_edge, cells_on_edge, edges_on_cell, send_cells,
    level_coef,
):
    length = send_cells.shape[1]
    fields_n, levels_n, cell_count = field.shape
    edge_count = dv_edge.shape[0]
    _, _, used = slots(length)
    halo = up(used, LANES)
    stride = up(levels_n, 8)
    rows = up(fields_n * stride, CHUNKS * LANES)
    chunk = rows // CHUNKS
    vmem = pl.BlockSpec(memory_space=pltpu.VMEM)
    near, coef, cols = pl.pallas_call(
        prepare_kernel,
        out_shape=(
            jax.ShapeDtypeStruct((8, cell_count), jnp.int32),
            jax.ShapeDtypeStruct((8, cell_count), jnp.float32),
            jax.ShapeDtypeStruct((used, LANES), jnp.int32),
        ),
        in_specs=[vmem] * 6,
        out_specs=(vmem,) * 3,
        scratch_shapes=[
            pltpu.VMEM((1, up(edge_count, LANES)), jnp.float32),
            pltpu.VMEM((1, up(edge_count, LANES)), jnp.int32),
            pltpu.VMEM((8, cell_count), jnp.int32),
        ],
        compiler_params=pltpu.CompilerParams(vmem_limit_bytes=8 * 1024 * 1024),
        name="prepare",
    )(
        dv_edge.reshape(1, edge_count),
        dc_edge.reshape(1, edge_count),
        cells_on_edge,
        edges_on_cell,
        send_cells,
        cell_area.reshape(1, cell_count),
    )
    second = pl.pallas_call(
        functools.partial(main_kernel, devices, length),
        out_shape=jax.ShapeDtypeStruct((rows, cell_count), jnp.float32),
        in_specs=[pl.BlockSpec(memory_space=pl.ANY), vmem, vmem, vmem],
        out_specs=vmem,
        scratch_shapes=[
            pltpu.VMEM((fields_n, levels_n, cell_count), jnp.float32),
            pltpu.VMEM((rows, cell_count), jnp.float32),
            pltpu.VMEM((rows, cell_count), jnp.float32),
            pltpu.VMEM((3 * cell_count, cell_count), jnp.bfloat16),
            pltpu.VMEM((3 * halo, cell_count), jnp.bfloat16),
            pltpu.VMEM((CHUNKS, chunk, 3 * cell_count), jnp.bfloat16),
            pltpu.VMEM((used, 2 * cell_count), jnp.bfloat16),
            pltpu.VMEM((2, CHUNKS, used, chunk), jnp.float32),
            pltpu.VMEM((2, CHUNKS, halo, chunk), jnp.float32),
            pltpu.SemaphoreType.DMA((fields_n,)),
            pltpu.SemaphoreType.DMA((2, CHUNKS, 6)),
            pltpu.SemaphoreType.DMA((2, CHUNKS, 6)),
        ],
        compiler_params=pltpu.CompilerParams(
            collective_id=0, has_side_effects=True, vmem_limit_bytes=44 * 1024 * 1024
        ),
        name="diffuse",
    )(field, near, coef, cols)
    second = second[: fields_n * stride].reshape(fields_n, stride, cell_count)[:, :levels_n]
    return -level_coef[None, :, None] * second


def solution(mesh):
    return jax.shard_map(
        functools.partial(shards, mesh.shape["cells"]),
        mesh=mesh,
        in_specs=(
            P(None, None, "cells"),
            P("cells"),
            P("cells"),
            P("cells"),
            P(None, "cells"),
            P(None, "cells"),
            P(None, "cells"),
            P(),
        ),
        out_specs=P(None, None, "cells"),
        check_vma=False,
    )
```

time: 233 us -> 46.4 us (0.20)
  matrix products: 124 us -> 0 us
  local copies, waits for them, and re-layouts: 56.5 us -> 6.54 us
  Pallas kernels: 0 us -> 37.8 us
  starting transfers between devices: 26.7 us -> 0 us
  other arithmetic: 15.6 us -> 1.56 us
  waiting for transfers between devices: 9.76 us -> 0 us
    dot_general x5 -> x0, matrix products: 124 us -> none  [the longest x1 93.5 us: shards(): jnp.dot(differ, collect, precision=highest, preferred_element_type=jnp.fl...]
    pallas_call x0 -> x2, Pallas kernels: none -> 37.8 us  [the longest x1 37.2 us: shards(): pl.pallas_call(functools.partial(main_kernel, devices, length), out_shape...]
    gather x2 -> x0, local copies, waits for them, and re-layouts: 34.3 us -> none  [shards(): first_end = jnp.take(cells_on_edge[0], edges_on_cell)]
    ppermute x8 -> x0, starting transfers between devices: 26.7 us -> none  [from_behind(): lax.ppermute(x, axis, [(i, (i + by) % devices) for i in range(devices)])]
    dot_general x1 -> x0, other arithmetic: 11.6 us -> none  [shards(): jnp.dot(differ, collect, precision=highest, preferred_element_type=jnp.fl...]
    ppermute x8 -> x0, waiting for transfers between devices: 9.76 us -> none  [from_behind(): lax.ppermute(x, axis, [(i, (i + by) % devices) for i in range(devices)])]
    concatenate x4 -> x0, local copies, waits for them, and re-layouts: 7.35 us -> none  [the longest x2 6.37 us: extend(): jnp.concatenate([values, widen(from_left, length), widen(from_right, leng...]
    slice x18 -> x1, local copies, waits for them, and re-layouts: 5.87 us -> 0.13 us  [shards(): second[:fields_n * stride].reshape(fields_n, stride, cell_count)]
  transfers between devices with their start and end apart: 8 -> 0, of which waited for: 4 -> 0; matrix products, arithmetic and copies ran while one was open for 63% -> 0% of each run, Pallas kernels for 0% -> 0%
where the time goes in v1:
time: 46.4 us; the launch traced here: 46 us
  Pallas kernels  37.8 us (81%)
  local copies, waits for them, and re-layouts  6.54 us (14%)
  other arithmetic  1.56 us (3%)
    pallas_call x1, Pallas kernels, shards(): pl.pallas_call(functools.partial(main_kernel, devices, length), out_shape...  37.2 us
    unnamed x12, local copies, waits for them, and re-layouts  4.95 us
    mul x1, other arithmetic, shards(): return -level_coef[None, :, None] * second  1.56 us

profile of v1, /device:TPU:0, one launch (start us, length us, event | category | flops | bytes accessed | tf_op | source)
XLA Modules:
  0.0 46.0 jit_solution(786162417484389008)
XLA Ops:
  0.0 0.7 %reshape.14.dv_ref = f32[1,3232]{1,0:T(1,128)S(1)} reshape(f32[3232]{0:T(1024)} %param.10) | data formatting | bytes 25856 | tf_op jit(solution)/shard_map/reshape | solution.py:266
  0.7 0.7 %reshape.15.dc_ref = f32[1,3232]{1,0:T(1,128)S(1)} reshape(f32[3232]{0:T(1024)} %param.11) | data formatting | bytes 25856 | tf_op jit(solution)/shard_map/reshape | solution.py:267
  1.5 0.0 copy-start.1
  1.5 0.7 %copy-done.1 = s32[6,1024]{1,0:T(8,128)S(1)} copy-done((s32[6,1024]{1,0:T(8,128)S(1)}, s32[6,1024]{1,0:T(8,128)}, u32[]{:S(2)}) %copy-start.1) | copy-done | bytes 24600
  2.2 0.0 copy-start.2
  2.2 0.7 %copy-done.2 = s32[2,3232]{1,0:T(2,128)S(1)} copy-done((s32[2,3232]{1,0:T(2,128)S(1)}, s32[2,3232]{1,0:T(2,128)}, u32[]{:S(2)}) %copy-start.2) | copy-done | bytes 25880
  3.0 0.0 copy-start.3
  3.0 0.7 %copy-done.3 = s32[6,64]{1,0:T(8,128)S(1)} copy-done((s32[6,64]{1,0:T(8,128)S(1)}, s32[6,64]{1,0:T(8,128)}, u32[]{:S(2)}) %copy-start.3) | copy-done | bytes 1560
  3.7 0.0 copy-start.4
  3.7 0.7 %copy-done.4 = f32[1024]{0:T(1024)S(1)} copy-done((f32[1024]{0:T(1024)S(1)}, f32[1024]{0:T(1024)}, u32[]{:S(2)}) %copy-start.4) | copy-done | bytes 4120
  4.3 0.6 %prepare.1 = (s32[8,1024]{1,0:T(8,128)S(1)}, f32[8,1024]{1,0:T(8,128)S(1)}, s32[176,128]{1,0:T(8,128)S(1)}) custom-call(f32[1,3232]{1,0:T(1,128)S(1)} %reshape.14.dv_ref, f32[1,3232]{1,0:T(1,128)S(1)} %reshape.15.dc_ref, s32[2,3232]{1,0:T(2,128)S(1)} %copy-done.2, s32[6,1024]{1,0:T(8,128)S(1)} %copy-done.1, s32[6,64]{1,0:T(8,128)S(1)} %copy-done.3, ...), custom_call_target="tpu_custom_call" | custom-call | tf_op jit(solution)/shard_map/prepare/pallas_call | solution.py:249
  4.9 0.0 copy-start
  4.9 1.6 %copy-done = f32[9,55,1024]{2,1,0:T(8,128)S(1)} copy-done((f32[9,55,1024]{2,1,0:T(8,128)S(1)}, f32[9,55,1024]{2,1,0:T(8,128)}, u32[]{:S(2)}) %copy-start) | copy-done | bytes 2027544
  6.5 37.2 %diffuse.1 = f32[512,1024]{1,0:T(8,128)S(1)} custom-call(f32[9,55,1024]{2,1,0:T(8,128)S(1)} %copy-done, s32[8,1024]{1,0:T(8,128)S(1)} %get-tuple-element.8.near_ref, f32[8,1024]{1,0:T(8,128)S(1)} %get-tuple-element.9.coef_ref, s32[176,128]{1,0:T(8,128)S(1)} %get-tuple-element.10.cols_ref), custom_call_target="tpu_custom_call" | custom-call | tf_op jit(solution)/shard_map/diffuse/pallas_call | solution.py:273
  43.7 0.0 copy-start.5
  43.7 0.1 slice.6
  43.9 0.5 %copy-done.5 = f32[55]{0:T(128)S(1)} copy-done((f32[55]{0:T(128)S(1)}, f32[55]{0:T(128)}, u32[]{:S(2)}) %copy-start.5) | copy-done | bytes 244
  44.4 1.6 %slice_multiply_fusion = f32[9,55,1024]{2,1,0:T(8,128)} fusion(f32[9,56,1024]{2,1,0:T(8,128)S(1)} %bitcast.3, f32[55]{0:T(128)S(1)} %neg.4), kind=kLoop, calls=%fused_computation | loop fusion | flops 506880 | bytes 4055260 | tf_op jit(solution)/shard_map/mul | solution.py:298
  (1 shorter events, 0.0 us)
Async XLA Ops:
  1.5 0.8 %copy-start.1 = (s32[6,1024]{1,0:T(8,128)S(1)}, s32[6,1024]{1,0:T(8,128)}, u32[]{:S(2)}) copy-start(s32[6,1024]{1,0:T(8,128)} %edges_ref.1) | copy-start | bytes 73732
  2.2 0.7 %copy-start.2 = (s32[2,3232]{1,0:T(2,128)S(1)}, s32[2,3232]{1,0:T(2,128)}, u32[]{:S(2)}) copy-start(s32[2,3232]{1,0:T(2,128)} %ends_ref.1) | copy-start | bytes 77572
  3.0 0.7 %copy-start.3 = (s32[6,64]{1,0:T(8,128)S(1)}, s32[6,64]{1,0:T(8,128)}, u32[]{:S(2)}) copy-start(s32[6,64]{1,0:T(8,128)} %send_ref.1) | copy-start | bytes 4612
  3.7 0.7 %copy-start.4 = (f32[1024]{0:T(1024)S(1)}, f32[1024]{0:T(1024)}, u32[]{:S(2)}) copy-start(f32[1024]{0:T(1024)} %param.9) | copy-start | bytes 12292
  4.9 1.6 %copy-start = (f32[9,55,1024]{2,1,0:T(8,128)S(1)}, f32[9,55,1024]{2,1,0:T(8,128)}, u32[]{:S(2)}) copy-start(f32[9,55,1024]{2,1,0:T(8,128)} %field_ref.1) | copy-start | bytes 6082564
  43.7 0.7 %copy-start.5 = (f32[55]{0:T(128)S(1)}, f32[55]{0:T(128)}, u32[]{:S(2)}) copy-start(f32[55]{0:T(128)} %param.15) | copy-start | bytes 664

commit v2 on v1

--- a/solution.py
+++ b/solution.py
@@ -31,10 +31,17 @@
 
 
 def prepare_kernel(
-    dv_ref, dc_ref, ends_ref, edges_ref, send_ref, area_ref, near_ref, coef_ref, cols_ref,
-    weight, packed, index,
+    dv_hbm, dc_hbm, ends_hbm, edges_hbm, send_hbm, area_hbm, near_ref, coef_ref, cols_ref,
+    weight, packed, index, dv_ref, dc_ref, ends_ref, edges_ref, send_ref, area_ref, sems,
 ):
-    edge_count = dv_ref.shape[1]
+    pairs = (
+        (dv_hbm, dv_ref), (dc_hbm, dc_ref), (ends_hbm, ends_ref), (edges_hbm, edges_ref),
+        (send_hbm, send_ref), (area_hbm, area_ref),
+    )
+    loads = [pltpu.make_async_copy(a, b, sems.at[i]) for i, (a, b) in enumerate(pairs)]
+    for load in loads:
+        load.start()
+    edge_count = ends_ref.shape[1]
     cell_count = edges_ref.shape[1]
     length = send_ref.shape[1]
     base, counts, _ = slots(length)
@@ -42,7 +49,11 @@
     weight[...] = jnp.zeros_like(weight)
     packed[...] = jnp.zeros_like(packed)
     index[...] = jnp.zeros_like(index)
-    weight[:, :edge_count] = dv_ref[...] / dc_ref[...]
+    for load in loads:
+        load.wait()
+    for k in range(tables):
+        part = slice(k * LANES, min((k + 1) * LANES, edge_count))
+        weight[0, part] = dv_ref[part] / dc_ref[part]
     packed[:, :edge_count] = ends_ref[0:1, :] + ends_ref[1:2, :] * 4096
     index[0:6, :] = edges_ref[...]
     row = lax.broadcasted_iota(jnp.int32, (8, LANES), 0)
@@ -70,7 +81,7 @@
             inside = (away >= k * length) & (away < (k + 1) * length)
             place = jnp.where(inside, away - k * length + base[k], place)
         near = jnp.where(away < 0, other, cell_count + place)
-        share = w / area_ref[0:1, here]
+        share = w / jnp.broadcast_to(area_ref[here], (8, LANES))
         share = jnp.where(row < 6, share, 0.0)
         total = jnp.sum(share, axis=0, keepdims=True)
         near_ref[:, here] = jnp.where(row < 6, near, -1)
@@ -246,6 +257,7 @@
     rows = up(fields_n * stride, CHUNKS * LANES)
     chunk = rows // CHUNKS
     vmem = pl.BlockSpec(memory_space=pltpu.VMEM)
+    hbm = pl.BlockSpec(memory_space=pltpu.HBM)
     near, coef, cols = pl.pallas_call(
         prepare_kernel,
         out_shape=(
@@ -253,27 +265,34 @@
             jax.ShapeDtypeStruct((8, cell_count), jnp.float32),
             jax.ShapeDtypeStruct((used, LANES), jnp.int32),
         ),
-        in_specs=[vmem] * 6,
+        in_specs=[hbm] * 6,
         out_specs=(vmem,) * 3,
         scratch_shapes=[
             pltpu.VMEM((1, up(edge_count, LANES)), jnp.float32),
             pltpu.VMEM((1, up(edge_count, LANES)), jnp.int32),
             pltpu.VMEM((8, cell_count), jnp.int32),
+            pltpu.VMEM(dv_edge.shape, jnp.float32),
+            pltpu.VMEM(dc_edge.shape, jnp.float32),
+            pltpu.VMEM(cells_on_edge.shape, jnp.int32),
+            pltpu.VMEM(edges_on_cell.shape, jnp.int32),
+            pltpu.VMEM(send_cells.shape, jnp.int32),
+            pltpu.VMEM(cell_area.shape, jnp.float32),
+            pltpu.SemaphoreType.DMA((6,)),
         ],
-        compiler_params=pltpu.CompilerParams(vmem_limit_bytes=8 * 1024 * 1024),
+        compiler_params=pltpu.CompilerParams(vmem_limit_bytes=67043328),
         name="prepare",
     )(
-        dv_edge.reshape(1, edge_count),
-        dc_edge.reshape(1, edge_count),
+        dv_edge,
+        dc_edge,
         cells_on_edge,
         edges_on_cell,
         send_cells,
-        cell_area.reshape(1, cell_count),
+        cell_area,
     )
     second = pl.pallas_call(
         functools.partial(main_kernel, devices, length),
         out_shape=jax.ShapeDtypeStruct((rows, cell_count), jnp.float32),
-        in_specs=[pl.BlockSpec(memory_space=pl.ANY), vmem, vmem, vmem],
+        in_specs=[hbm, vmem, vmem, vmem],
         out_specs=vmem,
         scratch_shapes=[
             pltpu.VMEM((fields_n, levels_n, cell_count), jnp.float32),

time: 46.4 us -> 45.9 us (0.989)
  local copies, waits for them, and re-layouts: 6.54 us -> 4.62 us
  Pallas kernels: 37.8 us -> 39.3 us
    pallas_call x1, Pallas kernels: 0.59 us -> 2.09 us  [shards(): pl.pallas_call(prepare_kernel, out_shape=(jax.ShapeDtypeStruct((8, cell_c...]
    reshape x2 -> x0, local copies, waits for them, and re-layouts: 1.46 us -> none  [the longest x1 0.73 us: shards(): dc_edge.reshape(1, edge_count)]
    unnamed x12 -> x10, local copies, waits for them, and re-layouts: 4.95 us -> 4.49 us
where the time goes in v2:
time: 45.9 us; the launch traced here: 45.5 us
  Pallas kernels  39.3 us (86%)
  local copies, waits for them, and re-layouts  4.62 us (10%)
  other arithmetic  1.56 us (3%)
    pallas_call x1, Pallas kernels, shards(): pl.pallas_call(functools.partial(main_kernel, devices, length), out_shape...  37.2 us
    unnamed x10, local copies, waits for them, and re-layouts  4.49 us
    pallas_call x1, Pallas kernels, shards(): pl.pallas_call(prepare_kernel, out_shape=(jax.ShapeDtypeStruct((8, cell_c...  2.09 us
    mul x1, other arithmetic, shards(): return -level_coef[None, :, None] * second  1.56 us

profile of v2, /device:TPU:0, one launch (start us, length us, event | category | flops | bytes accessed | tf_op | source)
XLA Modules:
  0.0 45.5 jit_solution(2256880559030441489)
XLA Ops:
  0.0 2.1 %prepare.1 = (s32[8,1024]{1,0:T(8,128)}, f32[8,1024]{1,0:T(8,128)}, s32[176,128]{1,0:T(8,128)}) custom-call(f32[3232]{0:T(1024)} %dv_hbm.1, f32[3232]{0:T(1024)} %dc_hbm.1, s32[2,3232]{1,0:T(2,128)} %ends_hbm.1, s32[6,1024]{1,0:T(8,128)} %edges_hbm.1, s32[6,64]{1,0:T(8,128)} %send_hbm.1, f32[1024]{0:T(1024)} %area_hbm.1), custom_call_target="tpu_custom_call" | custom-call | tf_op jit(solution)/shard_map/prepare/pallas_call | solution.py:261
  2.1 0.0 copy-start
  2.1 1.6 %copy-done = f32[9,55,1024]{2,1,0:T(8,128)S(1)} copy-done((f32[9,55,1024]{2,1,0:T(8,128)S(1)}, f32[9,55,1024]{2,1,0:T(8,128)}, u32[]{:S(2)}) %copy-start) | copy-done | bytes 2027544
  3.7 0.0 copy-start.1
  3.7 0.9 %copy-done.1 = s32[176,128]{1,0:T(8,128)S(1)} copy-done((s32[176,128]{1,0:T(8,128)S(1)}, s32[176,128]{1,0:T(8,128)}, u32[]{:S(2)}) %copy-start.1) | copy-done | bytes 90136
  4.6 0.0 copy-start.2
  4.6 0.8 %copy-done.2 = s32[8,1024]{1,0:T(8,128)S(1)} copy-done((s32[8,1024]{1,0:T(8,128)S(1)}, s32[8,1024]{1,0:T(8,128)}, u32[]{:S(2)}) %copy-start.2) | copy-done | bytes 32792
  5.3 0.0 copy-start.3
  5.3 0.8 %copy-done.3 = f32[8,1024]{1,0:T(8,128)S(1)} copy-done((f32[8,1024]{1,0:T(8,128)S(1)}, f32[8,1024]{1,0:T(8,128)}, u32[]{:S(2)}) %copy-start.3) | copy-done | bytes 32792
  6.1 37.2 %diffuse.1 = f32[512,1024]{1,0:T(8,128)S(1)} custom-call(f32[9,55,1024]{2,1,0:T(8,128)S(1)} %copy-done, s32[8,1024]{1,0:T(8,128)S(1)} %copy-done.2, f32[8,1024]{1,0:T(8,128)S(1)} %copy-done.3, s32[176,128]{1,0:T(8,128)S(1)} %copy-done.1), custom_call_target="tpu_custom_call" | custom-call | tf_op jit(solution)/shard_map/diffuse/pallas_call | solution.py:292
  43.3 0.0 copy-start.4
  43.3 0.1 slice.6
  43.5 0.5 %copy-done.4 = f32[55]{0:T(128)S(1)} copy-done((f32[55]{0:T(128)S(1)}, f32[55]{0:T(128)}, u32[]{:S(2)}) %copy-start.4) | copy-done | bytes 244
  44.0 1.6 %slice_multiply_fusion = f32[9,55,1024]{2,1,0:T(8,128)} fusion(f32[9,56,1024]{2,1,0:T(8,128)S(1)} %bitcast.1, f32[55]{0:T(128)S(1)} %neg.4), kind=kLoop, calls=%fused_computation | loop fusion | flops 506880 | bytes 4055260 | tf_op jit(solution)/shard_map/mul | solution.py:317
  (1 shorter events, 0.0 us)
Async XLA Ops:
  2.1 1.6 %copy-start = (f32[9,55,1024]{2,1,0:T(8,128)S(1)}, f32[9,55,1024]{2,1,0:T(8,128)}, u32[]{:S(2)}) copy-start(f32[9,55,1024]{2,1,0:T(8,128)} %field_ref.1) | copy-start | bytes 6082564
  3.7 0.9 %copy-start.1 = (s32[176,128]{1,0:T(8,128)S(1)}, s32[176,128]{1,0:T(8,128)}, u32[]{:S(2)}) copy-start(s32[176,128]{1,0:T(8,128)} %get-tuple-element.10.cols_ref) | copy-start | bytes 270340
  4.6 0.8 %copy-start.2 = (s32[8,1024]{1,0:T(8,128)S(1)}, s32[8,1024]{1,0:T(8,128)}, u32[]{:S(2)}) copy-start(s32[8,1024]{1,0:T(8,128)} %get-tuple-element.8.near_ref) | copy-start | bytes 98308
  5.3 0.8 %copy-start.3 = (f32[8,1024]{1,0:T(8,128)S(1)}, f32[8,1024]{1,0:T(8,128)}, u32[]{:S(2)}) copy-start(f32[8,1024]{1,0:T(8,128)} %get-tuple-element.9.coef_ref) | copy-start | bytes 98308
  43.3 0.7 %copy-start.4 = (f32[55]{0:T(128)S(1)}, f32[55]{0:T(128)}, u32[]{:S(2)}) copy-start(f32[55]{0:T(128)} %param.15) | copy-start | bytes 664
